TPU v7x, 32 devices: a whole 2x2x4 slice. The times are simulated.
32 devices in a mesh: row: 4 (over y, x), col: 8 (over z, core).
Axes of the slice: x: 2, y: 2, z: 4, core: 2. Of those that a mesh axis runs over, the one named last changes fastest.
Arguments:
- gradient: bfloat16 [2304, 18432], P('row', 'col'), may hold values from -6 to 6
- left_basis: bfloat16 [2304, 2304], P('row'), may hold values from -0.125 to 0.125
- right_basis: bfloat16 [18432, 18432], P('col', 'row'), may hold values from -0.046875 to 0.046875
- first_moment: float32 [2304, 18432], P('col', 'row'), may hold values from -3 to 3
- second_moment: float32 [2304, 18432], P('col', 'row'), may hold values from 0.25 to 4
Outputs:
- update: bfloat16 [2304, 18432], P('row', 'col')
- first_new: float32 [2304, 18432], P('col', 'row')
- second_new: float32 [2304, 18432], P('col', 'row')
All inputs are finite; a program needn't handle non-finite values.
Results may differ from a plain program's by a relative error of at most 0.018.
Values may be sent and summed in bfloat16 or wider, within the bound.
A program may use at most 128 MiB of HBM per device.

v0:
```python
import jax
import jax.numpy as jnp
from jax import lax
from jax.sharding import PartitionSpec as P

beta_one = 0.9
beta_two = 0.95
epsilon = 1e-08
correct_one = 1.0 - 0.9**10
correct_two = 1.0 - 0.95**10


def per_device(gradient, left_basis, right_basis, first_moment, second_moment):
    partial_value = lax.dot_general(
        left_basis, gradient, (((0,), (0,)), ((), ())), preferred_element_type=jnp.float32
    )
    rotated_left = lax.psum(partial_value.astype(jnp.bfloat16), "row")
    rotated = lax.psum_scatter(
        jnp.dot(rotated_left, right_basis, preferred_element_type=jnp.float32).astype(jnp.bfloat16),
        "col",
        scatter_dimension=0,
        tiled=True,
    )
    rotated_wide = rotated.astype(jnp.float32)
    first_new = beta_one * first_moment + (1.0 - beta_one) * rotated_wide
    second_new = beta_two * second_moment + (1.0 - beta_two) * rotated_wide * rotated_wide
    step_rot = (first_new / correct_one / (jnp.sqrt(second_new / correct_two) + epsilon)).astype(
        jnp.bfloat16
    )
    back_part = lax.dot_general(
        lax.all_gather(step_rot, "col", axis=0, tiled=True),
        right_basis,
        (((1,), (1,)), ((), ())),
        preferred_element_type=jnp.float32,
    )
    back_own = lax.psum_scatter(
        back_part.astype(jnp.bfloat16), "row", scatter_dimension=0, tiled=True
    )
    back_rot = lax.all_gather(back_own, "row", axis=0, tiled=True)
    update = jnp.dot(left_basis, back_rot, preferred_element_type=jnp.float32).astype(jnp.bfloat16)
    return (update, first_new, second_new)


def solution(mesh):
    in_specs = (P("row", "col"), P("row", None), P("col", "row"), P("col", "row"), P("col", "row"))
    out_specs = (P("row", "col"), P("col", "row"), P("col", "row"))
    return jax.shard_map(
        per_device, mesh=mesh, in_specs=in_specs, out_specs=out_specs, check_vma=False
    )
```

profile of v0, /device:TPU:0, one launch (start us, length us, event | category | flops | bytes accessed | tf_op | source)
XLA Modules:
  0.0 982.5 jit_solution(14175952818253568337)
XLA Ops:
  7.2 0.0 copy-start
  7.2 0.0 all-reduce.2.cloned.1.call-start
  7.2 1.7 copy-done
  8.9 12.5 %convolution_convert_fusion.2 = bf16[2304,2304]{1,0:T(8,128)(2,1)} fusion(bf16[576,2304]{1,0:T(8,128)(2,1)S(1)} %copy-done, bf16[576,2304]{1,0:T(8,128)(2,1)} %param.5), kind=kOutput, calls=%fused_computation.2 | convolution fusion | flops 6120603648 | bytes 15925248 | tf_op jit(solution)/shard_map/dot_general | solution.py:14
  21.4 0.0 all-reduce.2.cloned.1.call-update
  21.4 0.0 reduce-scatter.3.cloned.1.call-start
  21.5 210.5 %all-reduce.2.cloned.1.call-done = bf16[2304,2304]{1,0:T(8,128)(2,1)} async-done(((bf16[2304,2304]{1,0:T(8,128)(2,1)}), bf16[2304,2304]{1,0:T(8,128)(2,1)}) %all-reduce.2.cloned.1.call-update) | async-done | bytes 10616848 | tf_op jit(solution)/shard_map/psum | solution.py:17
  232.0 57.8 %convolution_convert_fusion = bf16[2304,4608]{1,0:T(8,128)(2,1)} fusion(bf16[2304,2304]{1,0:T(8,128)(2,1)} %all-reduce.2.cloned.1.call-done, bf16[2304,4608]{1,0:T(8,128)(2,1)} %param.7), kind=kOutput, calls=%fused_computation | convolution fusion | flops 48932978688 | bytes 53084160 | tf_op jit(solution)/shard_map/dot_general | solution.py:19
  289.7 0.0 reduce-scatter.3.cloned.1.call-update
  289.8 0.2 all-gather.3.cloned.1.call-start
  290.0 210.0 %reduce-scatter.3.cloned.1.call-done = bf16[288,4608]{1,0:T(8,128)(2,1)} async-done(((bf16[2304,4608]{1,0:T(8,128)(2,1)}), bf16[288,4608]{1,0:T(8,128)(2,1)}) %reduce-scatter.3.cloned.1.call-update) | async-done | bytes 2654224 | tf_op jit(solution)/shard_map/reduce_scatter | solution.py:18
  500.0 9.4 divide_convert_fusion
  509.4 0.0 all-gather.3.cloned.1.call-update
  509.4 0.0 reduce-scatter.5.cloned.1.call-start
  509.5 186.2 %all-gather.3.cloned.1.call-done = bf16[2304,4608]{1,0:T(8,128)(2,1)} async-done(((bf16[288,4608]{1,0:T(8,128)(2,1)}), bf16[2304,4608]{1,0:T(8,128)(2,1)}) %all-gather.3.cloned.1.call-update) | async-done | bytes 21233680 | tf_op jit(solution)/shard_map/all_gather | solution.py:31
  695.7 58.1 %convolution_convert_fusion.1 = bf16[2304,2304]{1,0:T(8,128)(2,1)} fusion(bf16[2304,4608]{1,0:T(8,128)(2,1)} %all-gather.3.cloned.1.call-done, bf16[2304,4608]{1,0:T(8,128)(2,1)} %param.7), kind=kOutput, calls=%fused_computation.1 | convolution fusion | flops 48927670272 | bytes 53084160 | tf_op jit(solution)/shard_map/dot_general | solution.py:30
  753.7 0.0 reduce-scatter.5.cloned.1.call-update
  753.8 0.0 all-gather.5.cloned.1.call-start
  753.8 102.8 %reduce-scatter.5.cloned.1.call-done = bf16[576,2304]{1,0:T(8,128)(2,1)} async-done(((bf16[2304,2304]{1,0:T(8,128)(2,1)}), bf16[576,2304]{1,0:T(8,128)(2,1)}) %reduce-scatter.5.cloned.1.call-update) | async-done | bytes 2654224 | tf_op jit(solution)/shard_map/reduce_scatter | solution.py:36
  856.6 0.0 all-gather.5.cloned.1.call-update
  856.7 107.7 %all-gather.5.cloned.1.call-done = bf16[2304,2304]{1,0:T(8,128)(2,1)} async-done(((bf16[576,2304]{1,0:T(8,128)(2,1)}), bf16[2304,2304]{1,0:T(8,128)(2,1)}) %all-gather.5.cloned.1.call-update) | async-done | bytes 10616848 | tf_op jit(solution)/shard_map/all_gather | solution.py:39
  964.4 11.6 %fusion.2 = bf16[576,2304]{1,0:T(8,128)(2,1)} fusion(bf16[576,2304]{1,0:T(8,128)(2,1)S(1)} %copy-done, bf16[2304,2304]{1,0:T(8,128)(2,1)} %all-gather.5.cloned.1.call-done), kind=kOutput, calls=%fused_computation.9 | convolution fusion | flops 6116622336 | bytes 15925248 | tf_op jit(solution)/shard_map/dot_general | solution.py:40
Async XLA Ops:
  7.2 1.8 copy-start
  7.2 224.8 %all-reduce.2.cloned.1.call-start = ((), (), s32[]{:S(2)}) async-start(), calls=%async_computation.2 | async-start | bytes 21233664 | tf_op jit(solution)/shard_map/psum | solution.py:17
  21.4 478.6 %reduce-scatter.3.cloned.1.call-start = ((), (), s32[]{:S(2)}) async-start(), calls=%async_computation.3 | async-start | bytes 23887872 | tf_op jit(solution)/shard_map/reduce_scatter | solution.py:18
  289.8 405.9 %all-gather.3.cloned.1.call-start = ((), (), s32[]{:S(2)}) async-start(), calls=%async_computation.4 | async-start | bytes 23887872 | tf_op jit(solution)/shard_map/all_gather | solution.py:31
  509.4 347.2 %reduce-scatter.5.cloned.1.call-start = ((), (), s32[]{:S(2)}) async-start(), calls=%async_computation.5 | async-start | bytes 13271040 | tf_op jit(solution)/shard_map/reduce_scatter | solution.py:36
  753.8 210.6 %all-gather.5.cloned.1.call-start = ((), (), s32[]{:S(2)}) async-start(), calls=%async_computation.6 | async-start | bytes 13271040 | tf_op jit(solution)/shard_map/all_gather | solution.py:39
Sparse Core Ops, SparseCore 0:
  21.6 210.3 all-reduce.1
  289.9 210.0 reduce-scatter.2
  509.6 186.0 all-gather.2
  753.9 102.7 reduce-scatter.4
  858.3 106.0 all-gather.4
where the time goes:
time: 983 us
  waiting for transfers between devices  817 us (83%)
  matrix products  140 us (14%)
  between operations  13.8 us (1%)
    psum x1, waiting for transfers between devices, per_device(): rotated_left = lax.psum(partial_value.astype(jnp.bfloat16), 'row')  210 us
    reduce_scatter x1, waiting for transfers between devices, per_device(): lax.psum_scatter(jnp.dot(rotated_left, right_basis, preferred_element_typ...  210 us
    all_gather x1, waiting for transfers between devices, per_device(): lax.all_gather(step_rot, 'col', axis=0, tiled=True)  186 us
    all_gather x1, waiting for transfers between devices, per_device(): back_rot = lax.all_gather(back_own, 'row', axis=0, tiled=True)  108 us
    reduce_scatter x1, waiting for transfers between devices, per_device(): lax.psum_scatter(back_part.astype(jnp.bfloat16), 'row', scatter_dimension...  103 us
    dot_general x1, matrix products, per_device(): lax.dot_general(lax.all_gather(step_rot, 'col', axis=0, tiled=True), righ...  58.1 us
    dot_general x1, matrix products, per_device(): jnp.dot(rotated_left, right_basis, preferred_element_type=jnp.float32)  57.8 us
  transfers between devices with their start and end apart: 5, of which 5 were waited for; matrix products, arithmetic and copies ran while one was open for 0% of the time, Pallas kernels for 0%

commit v1 on v0

--- a/solution.py
+++ b/solution.py
@@ -10,11 +10,16 @@
 correct_two = 1.0 - 0.95**10
 
 
+def add_all(array, name):
+    parts = lax.all_gather(array, name)
+    return jnp.sum(parts, axis=0)
+
+
 def per_device(gradient, left_basis, right_basis, first_moment, second_moment):
     partial_value = lax.dot_general(
         left_basis, gradient, (((0,), (0,)), ((), ())), preferred_element_type=jnp.float32
     )
-    rotated_left = lax.psum(partial_value.astype(jnp.bfloat16), "row")
+    rotated_left = add_all(partial_value.astype(jnp.bfloat16), "row")
     rotated = lax.psum_scatter(
         jnp.dot(rotated_left, right_basis, preferred_element_type=jnp.float32).astype(jnp.bfloat16),
         "col",

time: 983 us -> 1180 us (1.20)
  waiting for transfers between devices: 817 us -> 981 us
  other arithmetic: 9.39 us -> 44.1 us
    all_gather x0 -> x1, waiting for transfers between devices: none -> 374 us  [add_all(): parts = lax.all_gather(array, name)]
    psum x1 -> x0, waiting for transfers between devices: 210 us -> none  [per_device(): rotated_left = lax.psum(partial_value.astype(jnp.bfloat16), 'row')]
    reduce_sum x0 -> x1, other arithmetic: none -> 34.7 us  [add_all(): return jnp.sum(parts, axis=0)]
where the time goes in v1:
time: 1180 us
  waiting for transfers between devices  981 us (83%)
  matrix products  140 us (12%)
  other arithmetic  44.1 us (4%)
  between operations  13.8 us (1%)
    all_gather x1, waiting for transfers between devices, add_all(): parts = lax.all_gather(array, name)  374 us
    reduce_scatter x1, waiting for transfers between devices, per_device(): lax.psum_scatter(jnp.dot(rotated_left, right_basis, preferred_element_typ...  210 us
    all_gather x1, waiting for transfers between devices, per_device(): lax.all_gather(step_rot, 'col', axis=0, tiled=True)  186 us
    all_gather x1, waiting for transfers between devices, per_device(): back_rot = lax.all_gather(back_own, 'row', axis=0, tiled=True)  108 us
    reduce_scatter x1, waiting for transfers between devices, per_device(): lax.psum_scatter(back_part.astype(jnp.bfloat16), 'row', scatter_dimension...  103 us
    dot_general x1, matrix products, per_device(): lax.dot_general(lax.all_gather(step_rot, 'col', axis=0, tiled=True), righ...  58.1 us
    dot_general x1, matrix products, per_device(): jnp.dot(rotated_left, right_basis, preferred_element_type=jnp.float32)  57.8 us
    reduce_sum x1, other arithmetic, add_all(): return jnp.sum(parts, axis=0)  34.7 us
  transfers between devices with their start and end apart: 5, of which 5 were waited for; matrix products, arithmetic and copies ran while one was open for 0% of the time, Pallas kernels for 0%

profile of v1, /device:TPU:0, one launch (start us, length us, event | category | flops | bytes accessed | tf_op | source)
XLA Modules:
  0.0 1181.1 jit_solution(2363118378023920362)
XLA Ops:
  7.2 0.0 copy-start
  7.2 0.0 all-gather.9.cloned.1.call-start
  7.2 1.7 copy-done
  8.9 12.4 %convolution_convert_fusion.2 = bf16[2304,2304]{1,0:T(8,128)(2,1)} fusion(bf16[576,2304]{1,0:T(8,128)(2,1)S(1)} %copy-done, bf16[576,2304]{1,0:T(8,128)(2,1)} %param.5), kind=kOutput, calls=%fused_computation.2 | convolution fusion | flops 6120603648 | bytes 15925248 | tf_op jit(solution)/shard_map/dot_general | solution.py:19
  21.3 0.0 all-gather.9.cloned.1.call-update
  21.4 0.2 reduce-scatter.3.cloned.1.call-start
  21.6 374.3 %all-gather.9.cloned.1.call-done = bf16[9216,2304]{1,0:T(8,128)(2,1)} async-done(((bf16[2304,2304]{1,0:T(8,128)(2,1)}), bf16[9216,2304]{1,0:T(8,128)(2,1)}) %all-gather.9.cloned.1.call-update) | async-done | bytes 42467344 | tf_op jit(solution)/shard_map/all_gather | solution.py:14
  395.9 34.7 %reduce_sum.12 = bf16[2304,2304]{1,0:T(8,128)(2,1)} reduce(bf16[4,2304,2304]{2,1,0:T(8,128)(2,1)} %bitcast.11, bf16[]{:T(256)} %constant.4.clone.1), dimensions={0}, to_apply=%region_0.0 | reduce | flops 15925248 | bytes 53084160 | tf_op jit(solution)/shard_map/reduce_sum | solution.py:15
  430.6 57.8 %convolution_convert_fusion = bf16[2304,4608]{1,0:T(8,128)(2,1)} fusion(bf16[2304,2304]{1,0:T(8,128)(2,1)} %reduce_sum.12, bf16[2304,4608]{1,0:T(8,128)(2,1)} %param.7), kind=kOutput, calls=%fused_computation | convolution fusion | flops 48932978688 | bytes 53084160 | tf_op jit(solution)/shard_map/dot_general | solution.py:24
  488.4 0.0 reduce-scatter.3.cloned.1.call-update
  488.4 0.3 all-gather.5.cloned.1.call-start
  488.7 210.0 %reduce-scatter.3.cloned.1.call-done = bf16[288,4608]{1,0:T(8,128)(2,1)} async-done(((bf16[2304,4608]{1,0:T(8,128)(2,1)}), bf16[288,4608]{1,0:T(8,128)(2,1)}) %reduce-scatter.3.cloned.1.call-update) | async-done | bytes 2654224 | tf_op jit(solution)/shard_map/reduce_scatter | solution.py:23
  698.7 9.4 divide_convert_fusion
  708.1 0.0 all-gather.5.cloned.1.call-update
  708.1 0.0 reduce-scatter.5.cloned.1.call-start
  708.1 186.2 %all-gather.5.cloned.1.call-done = bf16[2304,4608]{1,0:T(8,128)(2,1)} async-done(((bf16[288,4608]{1,0:T(8,128)(2,1)}), bf16[2304,4608]{1,0:T(8,128)(2,1)}) %all-gather.5.cloned.1.call-update) | async-done | bytes 21233680 | tf_op jit(solution)/shard_map/all_gather | solution.py:36
  894.3 58.1 %convolution_convert_fusion.1 = bf16[2304,2304]{1,0:T(8,128)(2,1)} fusion(bf16[2304,4608]{1,0:T(8,128)(2,1)} %all-gather.5.cloned.1.call-done, bf16[2304,4608]{1,0:T(8,128)(2,1)} %param.7), kind=kOutput, calls=%fused_computation.1 | convolution fusion | flops 48927670272 | bytes 53084160 | tf_op jit(solution)/shard_map/dot_general | solution.py:35
  952.4 0.0 reduce-scatter.5.cloned.1.call-update
  952.4 0.0 all-gather.7.cloned.1.call-start
  952.5 102.8 %reduce-scatter.5.cloned.1.call-done = bf16[576,2304]{1,0:T(8,128)(2,1)} async-done(((bf16[2304,2304]{1,0:T(8,128)(2,1)}), bf16[576,2304]{1,0:T(8,128)(2,1)}) %reduce-scatter.5.cloned.1.call-update) | async-done | bytes 2654224 | tf_op jit(solution)/shard_map/reduce_scatter | solution.py:41
  1055.3 0.0 all-gather.7.cloned.1.call-update
  1055.3 107.7 %all-gather.7.cloned.1.call-done = bf16[2304,2304]{1,0:T(8,128)(2,1)} async-done(((bf16[576,2304]{1,0:T(8,128)(2,1)}), bf16[2304,2304]{1,0:T(8,128)(2,1)}) %all-gather.7.cloned.1.call-update) | async-done | bytes 10616848 | tf_op jit(solution)/shard_map/all_gather | solution.py:44
  1163.0 11.6 fusion.2
Async XLA Ops:
  7.2 1.8 copy-start
  7.2 388.8 %all-gather.9.cloned.1.call-start = ((), (), s32[]{:S(2)}) async-start(), calls=%async_computation.6 | async-start | bytes 53084160 | tf_op jit(solution)/shard_map/all_gather | solution.py:14
  21.4 677.3 %reduce-scatter.3.cloned.1.call-start = ((), (), s32[]{:S(2)}) async-start(), calls=%async_computation.2 | async-start | bytes 23887872 | tf_op jit(solution)/shard_map/reduce_scatter | solution.py:23
  488.4 405.9 %all-gather.5.cloned.1.call-start = ((), (), s32[]{:S(2)}) async-start(), calls=%async_computation.3 | async-start | bytes 23887872 | tf_op jit(solution)/shard_map/all_gather | solution.py:36
  708.1 347.2 %reduce-scatter.5.cloned.1.call-start = ((), (), s32[]{:S(2)}) async-start(), calls=%async_computation.4 | async-start | bytes 13271040 | tf_op jit(solution)/shard_map/reduce_scatter | solution.py:41
  952.4 210.6 %all-gather.7.cloned.1.call-start = ((), (), s32[]{:S(2)}) async-start(), calls=%async_computation.5 | async-start | bytes 13271040 | tf_op jit(solution)/shard_map/all_gather | solution.py:44
Sparse Core Ops, SparseCore 0:
  21.5 374.3 all-gather.8
  488.5 210.0 reduce-scatter.2
  708.2 186.0 all-gather.4
  952.5 102.7 reduce-scatter.4
  1057.0 106.0 all-gather.6
